TPU v7x, 32 devices: a whole 2x2x4 slice. The times are simulated.
32 devices in a mesh: wide: 2 (over x), narrow: 4 (over y, core), depth: 4 (over z).
Axes of the slice: x: 2, y: 2, z: 4, core: 2. Of those that a mesh axis runs over, the one named last changes fastest.
Arguments:
- patch_store: bfloat16 [8, 1024, 4096], P('wide', 'depth'), may hold values from -6 to 6
- w_key: bfloat16 [4096, 1024], P(None, 'narrow'), may hold values from -0.09375 to 0.09375
- w_value: bfloat16 [4096, 1024], P(None, 'narrow'), may hold values from -0.09375 to 0.09375
- key_gain: float32 [128], replicated, may hold values from 0.1 to 1.9
- query_gain: float32 [128], replicated, may hold values from 0.1 to 1.9
- queries: bfloat16 [32, 4096], P('wide', 'narrow'), may hold values from -6 to 6
- owner_table: int32 [8], replicated, may hold values from 0 to 7, each once
- reader_table: int32 [2, 2], replicated, may hold values from 0 to 7
- request_image: int32 [32], P('wide'), may hold values from 0 to 1
- image_tiles: int32 [8], replicated, may hold values from 1 to 4
Outputs:
- context: bfloat16 [32, 4096], P(('wide', 'depth'), 'narrow')
Inputs may be any that keep to these rules, and one draw needn't show every extreme that they name: owner_table is a permutation of the slots. `reader_table`: entries are image ids; a group's list may repeat an image.
All inputs are finite; a program needn't handle non-finite values.
Results may differ from a plain program's by a relative error of at most 0.012.
Values may be sent and summed in bfloat16 or wider, within the bound.
A program may use at most 64 MiB of HBM per device.

v0:
```python
import math

import jax
import jax.numpy as jnp
from jax import lax
from jax.sharding import PartitionSpec as P

HD = 128
TILE_P = 256


epsilon = 1e-05


def rms_scaled(tensor, scaling):
    return tensor / jnp.sqrt(jnp.mean(tensor * tensor, axis=-1, keepdims=True) + epsilon) * scaling


def local(
    patch_store,
    w_key,
    w_value,
    key_gain,
    query_gain,
    queries,
    owner_table,
    reader_table,
    request_image,
    image_tiles,
):
    images_here, rows_here, model_width = patch_store.shape
    kv_cols = w_key.shape[1]
    kv_local = kv_cols // HD
    patch_rows = patch_store.reshape(images_here * rows_here, model_width)
    key_rows = jnp.dot(patch_rows, w_key, preferred_element_type=jnp.float32).reshape(
        images_here, rows_here, kv_local, HD
    )
    key_rows = (
        rms_scaled(key_rows, key_gain)
        .astype(jnp.bfloat16)
        .reshape(images_here, rows_here * kv_cols)
    )
    values = jnp.dot(patch_rows, w_value, preferred_element_type=jnp.float32).astype(jnp.bfloat16)
    values = values.reshape(images_here, rows_here * kv_cols)
    owner_index = lax.axis_index("wide")
    wanted = owner_table[reader_table]
    read_count = reader_table.shape[1]
    batch_here = queries.shape[0]
    group_size = queries.shape[1] // (kv_local * HD)
    normed = rms_scaled(
        queries.astype(jnp.float32).reshape(batch_here, kv_local, group_size, HD), query_gain
    ).astype(jnp.bfloat16)
    row_ids = lax.axis_index("depth") * rows_here + jnp.arange(rows_here, dtype=jnp.int32)
    scale = 1.0 / math.sqrt(HD)
    local_slots = owner_index * images_here + jnp.arange(images_here, dtype=jnp.int32)
    picker = (wanted[:, :, None] == local_slots[None, None, :]).astype(jnp.bfloat16)
    send_keys = jnp.einsum(
        "wrj,jx->wrx", picker, key_rows, preferred_element_type=jnp.float32
    ).astype(jnp.bfloat16)
    send_values = jnp.einsum(
        "wrj,jx->wrx", picker, values, preferred_element_type=jnp.float32
    ).astype(jnp.bfloat16)
    got_keys, got_values = (
        lax.all_to_all(send_keys, "wide", split_axis=0, concat_axis=0, tiled=True),
        lax.all_to_all(send_values, "wide", split_axis=0, concat_axis=0, tiled=True),
    )
    read_keys = jnp.sum(got_keys, axis=0, dtype=jnp.float32).astype(jnp.bfloat16)
    read_values = jnp.sum(got_values, axis=0, dtype=jnp.float32).astype(jnp.bfloat16)
    read_keys = read_keys.reshape(read_count, rows_here, kv_local, HD)
    read_values = read_values.reshape(read_count, rows_here, kv_local, HD)
    scores = (
        jnp.einsum("bkgd,rskd->bkgrs", normed, read_keys, preferred_element_type=jnp.float32)
        * scale
    )
    my_images = reader_table[owner_index]
    chosen = (request_image[:, None] == jnp.arange(read_count, dtype=jnp.int32)[None, :]).astype(
        jnp.float32
    )
    usable = (row_ids[None, :] // TILE_P < image_tiles[my_images][:, None]).astype(jnp.float32)
    weights = jnp.exp(scores) * chosen[:, None, None, :, None] * usable[None, None, None]
    denominator = jnp.sum(weights, axis=(3, 4)).reshape(batch_here, kv_local * group_size)
    numerator = jnp.einsum(
        "bkgrs,rskd->bkgd",
        weights.astype(jnp.bfloat16),
        read_values,
        preferred_element_type=jnp.float32,
    )
    numerator = numerator.reshape(batch_here, kv_local * group_size * HD)
    row_share = batch_here // lax.axis_size("depth")
    numerator, denominator = (
        lax.psum(numerator.astype(jnp.bfloat16), "depth").astype(jnp.float32),
        lax.psum(denominator.astype(jnp.bfloat16), "depth").astype(jnp.float32),
    )
    first_row = lax.axis_index("depth") * row_share
    numerator = lax.dynamic_slice_in_dim(numerator, first_row, row_share, 0)
    denominator = lax.dynamic_slice_in_dim(denominator, first_row, row_share, 0)
    heads_here = denominator.shape[1]
    context = numerator.reshape(row_share, heads_here, HD) / denominator[:, :, None]
    return context.reshape(row_share, heads_here * HD).astype(jnp.bfloat16)


def solution(mesh):
    placed = (
        P("wide", "depth", None),
        P(None, "narrow"),
        P(None, "narrow"),
        P(),
        P(),
        P("wide", "narrow"),
        P(),
        P(),
        P("wide"),
        P(),
    )
    return jax.shard_map(
        local, mesh=mesh, in_specs=placed, out_specs=P(("wide", "depth"), "narrow"), check_vma=False
    )
```

profile of v0, /device:TPU:0, one launch (start us, length us, event | category | flops | bytes accessed | tf_op | source)
XLA Modules:
  0.0 63.2 jit_solution(15374107702283691047)
XLA Ops:
  0.0 4.3 %copy.48 = bf16[256,4096]{1,0:T(8,128)(2,1)} copy(bf16[256,4096]{0,1:T(8,128)(2,1)} %bitcast.51) | data formatting | bytes 4194304 | tf_op jit(solution)/shard_map/dot_general | solution.py:35
  4.3 6.4 %multiply_reduce_fusion = (f32[4,256,2]{1,2,0:T(2,128)S(1)}, f32[4,256,2,128]{1,3,2,0:T(8,128)S(1)}) fusion(bf16[2,128,4096,1]{2,1,0,3:T(8,128)(2,1)} %bitcast.52, bf16[4,256,4096]{2,1,0:T(8,128)(2,1)} %param.10), kind=kOutput, calls=%fused_computation.16 | convolution fusion | flops 2148005888 | bytes 11542528 | tf_op jit(solution)/shard_map/dot_general | solution.py:35
  10.7 0.1 multiply_convert_fusion
  10.8 0.4 copy.32
  11.3 0.2 reshape.199
  11.6 0.6 %gather_fusion = s32[4]{0:T(128)S(1)} fusion(s32[8]{0:T(128)S(1)} %copy-done.1, s32[1024]{0:T(1024)S(1)} %pad_clamp_fusion.1), kind=kCustom, calls=%fused_computation | custom fusion | bytes 48 | tf_op jit(solution)/shard_map/gather | solution.py:46
  12.3 1.4 %convolution_convert_fusion = bf16[2,2,65536]{2,1,0:T(2,128)(2,1)} fusion(bf16[4,65536,1]{1,0,2:T(4,128)(2,1)S(1)} %reshape.199, s32[4]{0:T(128)S(1)} %iota_add_fusion, s32[2,2]{1,0:T(2,128)S(1)} %reshape.179), kind=kOutput, calls=%fused_computation.2 | convolution fusion | flops 2359312 | bytes 1048608 | tf_op jit(solution)/shard_map/wrj,jx->wrx/dot_general | solution.py:57
  13.7 4.2 %all-to-all-start.1 = ((bf16[2,2,65536]{2,1,0:T(2,128)(2,1)}), bf16[2,2,65536]{2,1,0:T(2,128)(2,1)S(1)}, u32[]{:S(2)}, u32[]{:S(2)}) async-start(bf16[2,2,65536]{2,1,0:T(2,128)(2,1)} %convolution_convert_fusion), calls=%async_computation.1 | async-start | bytes 1048576 | tf_op jit(solution)/shard_map/all_to_all | solution.py:64
  18.0 0.1 multiply_reduce_fusion.1
  18.2 0.6 %gather_fusion.1 = s32[2]{0:T(128)S(1)} fusion(s32[8]{0:T(128)S(1)} %copy-done.2, s32[1024]{0:T(1024)S(1)} %pad_clamp_fusion), kind=kCustom, calls=%fused_computation.1 | custom fusion | bytes 24 | tf_op jit(solution)/shard_map/gather | solution.py:79
  18.9 6.5 %convolution_convert_fusion.2 = bf16[1024,256]{1,0:T(8,128)(2,1)} fusion(bf16[1024,4096]{1,0:T(8,128)(2,1)} %bitcast.56, bf16[4096,256]{1,0:T(8,128)(2,1)S(1)} %copy-done), kind=kOutput, calls=%fused_computation.6 | convolution fusion | flops 2147745792 | bytes 11010048 | tf_op jit(solution)/shard_map/dot_general | solution.py:43
  25.5 1.4 %reshape.196 = bf16[4,65536,1]{1,0,2:T(4,128)(2,1)S(1)} reshape(bf16[1024,256]{1,0:T(8,128)(2,1)} %convolution_convert_fusion.2) | data formatting | bytes 1048576 | tf_op jit(solution)/shard_map/reshape | solution.py:44
  26.9 1.4 %convolution_convert_fusion.1 = bf16[2,2,65536]{2,1,0:T(2,128)(2,1)} fusion(bf16[4,65536,1]{1,0,2:T(4,128)(2,1)S(1)} %reshape.196, s32[4]{0:T(128)S(1)} %iota_add_fusion, s32[2,2]{1,0:T(2,128)S(1)} %reshape.179), kind=kOutput, calls=%fused_computation.3 | convolution fusion | flops 2359312 | bytes 1048608 | tf_op jit(solution)/shard_map/wrj,jx->wrx/dot_general | solution.py:60
  28.3 3.5 %all-to-all-start = ((bf16[2,2,65536]{2,1,0:T(2,128)(2,1)}), bf16[2,2,65536]{2,1,0:T(2,128)(2,1)S(1)}, u32[]{:S(2)}, u32[]{:S(2)}) async-start(bf16[2,2,65536]{2,1,0:T(2,128)(2,1)} %convolution_convert_fusion.1), calls=%async_computation | async-start | bytes 1048576 | tf_op jit(solution)/shard_map/all_to_all | solution.py:65
  31.9 0.1 fusion.12
  32.0 1.1 %reduce_sum.53 = bf16[2,65536]{1,0:T(2,128)(2,1)S(1)} reduce(bf16[2,2,65536]{2,1,0:T(2,128)(2,1)S(1)} %all-to-all-done.1, bf16[]{:T(256)} %constant.16.clone.1), dimensions={0}, to_apply=%region_2.0 | reduce | flops 131072 | bytes 786434 | tf_op jit(solution)/shard_map/reduce_sum | solution.py:67
  33.2 0.2 reshape.173
  33.4 7.1 %all-to-all-done = bf16[2,2,65536]{2,1,0:T(2,128)(2,1)S(1)} async-done(((bf16[2,2,65536]{2,1,0:T(2,128)(2,1)}), bf16[2,2,65536]{2,1,0:T(2,128)(2,1)S(1)}, u32[]{:S(2)}, u32[]{:S(2)}) %all-to-all-start) | async-done | bytes 524320 | tf_op jit(solution)/shard_map/all_to_all | solution.py:65
  40.5 1.1 %reduce_sum.51 = bf16[2,65536]{1,0:T(2,128)(2,1)S(1)} reduce(bf16[2,2,65536]{2,1,0:T(2,128)(2,1)S(1)} %all-to-all-done, bf16[]{:T(256)} %constant.16.clone.1), dimensions={0}, to_apply=%region_0.0 | reduce | flops 131072 | bytes 786434 | tf_op jit(solution)/shard_map/reduce_sum | solution.py:68
  41.7 0.2 reshape.171
  41.9 0.3 fusion.22
  42.2 0.2 fusion.7
  42.4 19.9 %all-reduce = (bf16[16,8]{0,1:T(8,128)(2,1)S(1)}, bf16[16,1024]{1,0:T(8,128)(2,1)S(1)}) all-reduce(bf16[16,8]{0,1:T(8,128)(2,1)S(1)} %bitcast.55, bf16[16,1024]{1,0:T(8,128)(2,1)S(1)} %convert_element_type.72), channel_id=1, replica_groups=mesh['wide'=2,'narrow'=4,'depth'=4] {'depth'}, use_global_device_ids=true, to_apply=%region_6.7 | all-reduce | flops 16512 | bytes 66048 | tf_op jit(solution)/shard_map/psum | solution.py:92
  62.6 0.6 fusion.13
  (38 shorter events, 0.8 us)
Async XLA Ops:
  0.0 18.9 %copy-start = (bf16[4096,256]{1,0:T(8,128)(2,1)S(1)}, bf16[4096,256]{1,0:T(8,128)(2,1)}, u32[]{:S(2)}) copy-start(bf16[4096,256]{1,0:T(8,128)(2,1)} %param.12) | copy-start | bytes 6291460
  4.3 6.4 %copy-start.5 = (f32[128]{0:T(128)S(1)}, f32[128]{0:T(128)}, u32[]{:S(2)}) copy-start(f32[128]{0:T(128)} %param.13) | copy-start | bytes 1540
  10.6 0.8 %copy-start.4 = (s32[2,2]{1,0:T(2,128)S(1)}, s32[2,2]{1,0:T(2,128)}, u32[]{:S(2)}) copy-start(s32[2,2]{1,0:T(2,128)} %param.17) | copy-start | bytes 52
  10.7 0.9 %copy-start.1 = (s32[8]{0:T(128)S(1)}, s32[8]{0:T(128)}, u32[]{:S(2)}) copy-start(s32[8]{0:T(128)} %param.16) | copy-start | bytes 100
  11.3 6.7 %copy-start.3 = (bf16[16,1024]{1,0:T(8,128)(2,1)S(1)}, bf16[16,1024]{1,0:T(8,128)(2,1)}, u32[]{:S(2)}) copy-start(bf16[16,1024]{1,0:T(8,128)(2,1)} %param.15) | copy-start | bytes 98308
  11.3 7.0 %copy-start.2 = (s32[8]{0:T(128)S(1)}, s32[8]{0:T(128)}, u32[]{:S(2)}) copy-start(s32[8]{0:T(128)} %param.19) | copy-start | bytes 100
  13.7 14.6 %all-to-all-start.1 = ((bf16[2,2,65536]{2,1,0:T(2,128)(2,1)}), bf16[2,2,65536]{2,1,0:T(2,128)(2,1)S(1)}, u32[]{:S(2)}, u32[]{:S(2)}) async-start(bf16[2,2,65536]{2,1,0:T(2,128)(2,1)} %convolution_convert_fusion), calls=%async_computation.1 | async-start | bytes 1048576 | tf_op jit(solution)/shard_map/all_to_all | solution.py:64
  25.4 6.4 %copy-start.7 = (s32[16]{0:T(128)S(1)}, s32[16]{0:T(128)}, u32[]{:S(2)}) copy-start(s32[16]{0:T(128)} %param.18) | copy-start | bytes 196
  25.4 6.5 %copy-start.6 = (f32[128]{0:T(128)S(1)}, f32[128]{0:T(128)}, u32[]{:S(2)}) copy-start(f32[128]{0:T(128)} %param.14) | copy-start | bytes 1540
  28.3 12.2 %all-to-all-start = ((bf16[2,2,65536]{2,1,0:T(2,128)(2,1)}), bf16[2,2,65536]{2,1,0:T(2,128)(2,1)S(1)}, u32[]{:S(2)}, u32[]{:S(2)}) async-start(bf16[2,2,65536]{2,1,0:T(2,128)(2,1)} %convolution_convert_fusion.1), calls=%async_computation | async-start | bytes 1048576 | tf_op jit(solution)/shard_map/all_to_all | solution.py:65
where the time goes:
time: 63.5 us; the launch traced here: 63.2 us
  blocking collectives  19.9 us (31%)
  matrix products  16.1 us (25%)
  local copies, waits for them, and re-layouts  8.68 us (14%)
  starting transfers between devices  7.75 us (12%)
  waiting for transfers between devices  7.14 us (11%)
  other arithmetic  3.42 us (5%)
    psum x1, blocking collectives, local(): lax.psum(denominator.astype(jnp.bfloat16), 'depth').astype(jnp.float32)  19.9 us
    all_to_all x1, waiting for transfers between devices, local(): lax.all_to_all(send_values, 'wide', split_axis=0, concat_axis=0, tiled=True)  7.14 us
    dot_general x1, matrix products, local(): jnp.dot(patch_rows, w_value, preferred_element_type=jnp.float32)  6.52 us
    dot_general x1, matrix products, local(): jnp.dot(patch_rows, w_key, preferred_element_type=jnp.float32)  6.36 us
    dot_general x1, local copies, waits for them, and re-layouts, local(): jnp.dot(patch_rows, w_key, preferred_element_type=jnp.float32)  4.27 us
    all_to_all x1, starting transfers between devices, local(): lax.all_to_all(send_keys, 'wide', split_axis=0, concat_axis=0, tiled=True)  4.24 us
    all_to_all x1, starting transfers between devices, local(): lax.all_to_all(send_values, 'wide', split_axis=0, concat_axis=0, tiled=True)  3.51 us
    reshape x1, local copies, waits for them, and re-layouts, local(): values = values.reshape(images_here, rows_here * kv_cols)  1.44 us
  transfers between devices with their start and end apart: 2, of which 1 were waited for; matrix products, arithmetic and copies ran while one was open for 19% of the time, Pallas kernels for 0%

commit v1 on v0

v1 whole, which is shorter than its diff:
```python
import functools
import math

import jax
import jax.numpy as jnp
from jax import lax
from jax.experimental import pallas as pl
from jax.experimental.pallas import tpu as pltpu
from jax.sharding import PartitionSpec as P

HD = 128
TILE_P = 256
EPSILON = 1e-05
CHUNKS = 4
LAG = 3
MESH = pl.DeviceIdType.MESH


def kernel(
    n_wide,
    n_depth,
    store,
    w_key,
    w_value,
    key_gain,
    query_gain,
    queries,
    owner_table,
    reader_table,
    request_image,
    image_tiles,
    out,
    xbuf,
    wbuf,
    qraw,
    gains,
    qf,
    qs,
    qx,
    row_slot,
    row_limit,
    raw,
    acc,
    msg,
    got,
    res,
    w_sem,
    x0_sem,
    x_sem,
    q_sem,
    q_send,
    q_recv,
    m_send,
    m_recv,
):
    images, rows, width = xbuf.shape
    kv_local = wbuf.shape[0]
    batch = qraw.shape[0]
    group = qraw.shape[1] // (kv_local * HD)
    share = batch // n_depth
    block = share * group
    group_rows = n_depth * block
    peers = n_wide * n_depth
    total_rows = peers * block
    chunk = width // CHUNKS
    wide, depth = lax.axis_index("wide"), lax.axis_index("depth")
    me = wide * n_depth + depth

    def weight_copies(k, c):
        piece = pl.ds(c * chunk, chunk)
        return [
            pltpu.make_async_copy(
                source.at[piece, pl.ds(k * HD, HD)],
                wbuf.at[k, piece, pl.ds(part * HD, HD)],
                w_sem.at[k, c, part],
            )
            for part, source in enumerate((w_key, w_value))
        ]

    def first_copy(c):
        piece = pl.ds(c * chunk, chunk)
        return pltpu.make_async_copy(store.at[0, :, piece], xbuf.at[0, :, piece], x0_sem.at[c])

    def image_copy(j):
        return pltpu.make_async_copy(store.at[j], xbuf.at[j], x_sem.at[j])

    small = [
        pltpu.make_async_copy(queries, qraw, q_sem.at[0]),
        pltpu.make_async_copy(query_gain, gains.at[0], q_sem.at[1]),
        pltpu.make_async_copy(key_gain, gains.at[1], q_sem.at[2]),
    ]
    for c in range(CHUNKS):
        for copy in weight_copies(0, c):
            copy.start()
        first_copy(c).start()
        if c == 0:
            for copy in small:
                copy.start()
    for j in range(1, images):
        image_copy(j).start()
    for k in range(1, kv_local):
        for c in range(CHUNKS):
            for copy in weight_copies(k, c):
                copy.start()

    barrier = pltpu.get_barrier_semaphore()

    def peer(offset):
        index = lax.rem(me + offset, peers)
        return index, {"wide": index // n_depth, "depth": lax.rem(index, n_depth)}

    def greet(offset, carry):
        pl.semaphore_signal(barrier, inc=1, device_id=peer(offset)[1], device_id_type=MESH)
        return carry

    lax.fori_loop(1, peers, greet, 0, unroll=peers <= 8)

    for copy in small:
        copy.wait()
    gain = gains[0] * gains[1] * (1.0 / math.sqrt(HD))
    for h in range(kv_local * group):
        lanes = pl.ds(h * HD, HD)
        head = qraw[:, lanes].astype(jnp.float32)
        mean = jnp.mean(head * head, axis=-1, keepdims=True)
        qf[:, lanes] = head * lax.rsqrt(mean + EPSILON) * gain
    for k in range(kv_local):
        for t in range(n_depth):
            for g in range(group):
                qs[pl.ds(t * block + g * share, share), :] = qf[
                    pl.ds(t * share, share), pl.ds((k * group + g) * HD, HD)
                ]
        qx[wide, k] = qs[...].astype(jnp.bfloat16)
    row = lax.broadcasted_iota(jnp.int32, (group_rows, HD), 0)
    request = row // block * share + row % share
    entry = jnp.zeros((group_rows, HD), jnp.int32)
    for b in range(batch):
        entry = jnp.where(request == b, request_image[b], entry)
    qx[wide, kv_local] = entry.astype(jnp.float32).astype(jnp.bfloat16)
    acc[...] = jnp.zeros_like(acc)

    def query_copy(offset):
        return pltpu.make_async_remote_copy(
            src_ref=qx.at[wide],
            dst_ref=qx.at[wide],
            send_sem=q_send.at[offset],
            recv_sem=q_recv.at[offset],
            device_id={"wide": lax.rem(wide + offset, n_wide)},
            device_id_type=MESH,
        )

    def query_landed(offset):
        source = lax.rem(wide + n_wide - offset, n_wide)
        return pltpu.make_async_remote_copy(
            src_ref=qx.at[source],
            dst_ref=qx.at[source],
            send_sem=q_send.at[offset],
            recv_sem=q_recv.at[offset],
            device_id={"wide": lax.rem(wide + offset, n_wide)},
            device_id_type=MESH,
        )

    def result_copy(k, offset):
        index, device = peer(offset)
        return pltpu.make_async_remote_copy(
            src_ref=msg.at[k, index],
            dst_ref=got.at[k, offset],
            send_sem=m_send.at[k, offset],
            recv_sem=m_recv.at[k, offset],
            device_id=device,
            device_id_type=MESH,
        )

    def send_results(k):
        def step(offset, carry):
            result_copy(k, offset).start()
            return carry

        lax.fori_loop(1, peers, step, 0, unroll=peers <= 8)

    whole_tiles = TILE_P % rows == 0

    def read_queries():
        for offset in range(1, n_wide):
            query_landed(offset).wait_recv()
        for g in range(n_wide):
            entry = qx[g, kv_local].astype(jnp.float32)
            slots = jnp.full((group_rows, HD), -1, jnp.int32)
            limits = jnp.zeros((group_rows, HD), jnp.int32)
            for r in range(reader_table.shape[1]):
                image = reader_table[g, r]
                slot = owner_table[image]
                limit = image_tiles[image] * TILE_P - depth * rows
                if whole_tiles:
                    slot = jnp.where(limit > 0, slot, -1)
                slots = jnp.where(entry == r, slot, slots)
                limits = jnp.where(entry == r, limit, limits)
            row_slot[pl.ds(g * group_rows, group_rows), :] = slots
            row_limit[pl.ds(g * group_rows, group_rows), :] = limits

    def wider(tile):
        return jnp.concatenate([tile] * (rows // HD), axis=1) if rows > HD else tile

    def attend(unit):
        k, j = divmod(unit, images)
        keys = raw[unit, :, :HD]
        mean = jnp.mean(keys * keys, axis=-1, keepdims=True)
        keys = (keys * lax.rsqrt(mean + EPSILON)).astype(jnp.bfloat16)
        values = raw[unit, :, HD:].astype(jnp.bfloat16)
        values = jnp.concatenate([values, jnp.ones_like(values)], axis=1)
        asked = qx[:, k].reshape(total_rows, HD)
        scores = lax.dot_general(
            asked, keys, (((1,), (1,)), ((), ())), preferred_element_type=jnp.float32
        )
        keep = wider(row_slot[...]) == wide * images + j
        if not whole_tiles:
            place = lax.broadcasted_iota(jnp.int32, (total_rows, rows), 1)
            keep = keep & (place < wider(row_limit[...]))
        weights = jnp.where(keep, jnp.exp(scores), 0.0).astype(jnp.bfloat16)
        acc[k] += jnp.dot(weights, values, preferred_element_type=jnp.float32)
        if j == images - 1:
            msg[k] = acc[k].astype(jnp.bfloat16).reshape(peers, block, 2 * HD)

    def project(unit):
        k, j = divmod(unit, images)
        if unit == 0:
            total = jnp.zeros((rows, 2 * HD), jnp.float32)
            for c in range(CHUNKS):
                for copy in weight_copies(0, c):
                    copy.wait()
                first_copy(c).wait()
                piece = pl.ds(c * chunk, chunk)
                total = total + jnp.dot(
                    xbuf[0, :, piece], wbuf[0, piece, :], preferred_element_type=jnp.float32
                )
            raw[unit] = total
            return
        if k == 0:
            image_copy(j).wait()
        elif j == 0:
            for c in range(CHUNKS):
                for copy in weight_copies(k, c):
                    copy.wait()
        raw[unit] = jnp.dot(xbuf[j], wbuf[k], preferred_element_type=jnp.float32)

    units = kv_local * images
    pending, sent, ready = [], 0, []
    for unit in range(units):
        project(unit)
        if unit == 0:
            pl.semaphore_wait(barrier, peers - 1)
            for offset in range(1, n_wide):
                query_copy(offset).start()
        for k in ready:
            send_results(k)
        ready = []
        if unit == min(LAG, units - 1):
            read_queries()
        if unit >= LAG:
            for old in pending[:2]:
                attend(old)
                if old % images == images - 1:
                    ready.append(old // images)
            pending = pending[2:]
        pending.append(unit)
    for old in pending:
        attend(old)
        if old % images == images - 1:
            ready.append(old // images)
    for k in ready:
        send_results(k)

    for k in range(kv_local):
        total = msg[k, me].astype(jnp.float32)

        def collect(offset, total, k=k):
            result_copy(k, offset).wait_recv()
            return total + got[k, offset].astype(jnp.float32)

        total = lax.fori_loop(1, peers, collect, total, unroll=peers <= 8)
        res[...] = total[:, :HD] / total[:, HD:]
        for g in range(group):
            out[:, pl.ds((k * group + g) * HD, HD)] = res[pl.ds(g * share, share), :].astype(
                out.dtype
            )

    for offset in range(1, n_wide):
        query_copy(offset).wait_send()
    for k in range(kv_local):

        def drain(offset, carry, k=k):
            result_copy(k, offset).wait_send()
            return carry

        lax.fori_loop(1, peers, drain, 0, unroll=peers <= 8)


def local(
    n_wide,
    n_depth,
    patch_store,
    w_key,
    w_value,
    key_gain,
    query_gain,
    queries,
    owner_table,
    reader_table,
    request_image,
    image_tiles,
):
    images, rows, width = patch_store.shape
    kv_local = w_key.shape[1] // HD
    batch, q_cols = queries.shape
    group = q_cols // (kv_local * HD)
    share = batch // n_depth
    block = share * group
    group_rows = n_depth * block
    peers = n_wide * n_depth
    total_rows = peers * block
    anywhere = pl.BlockSpec(memory_space=pl.ANY)
    scalars = pl.BlockSpec(memory_space=pltpu.SMEM)
    dma = pltpu.SemaphoreType.DMA
    return pl.pallas_call(
        functools.partial(kernel, n_wide, n_depth),
        out_shape=jax.ShapeDtypeStruct((share, q_cols), jnp.bfloat16),
        in_specs=[anywhere] * 6 + [scalars] * 4,
        out_specs=pl.BlockSpec(memory_space=pltpu.VMEM),
        scratch_shapes=[
            pltpu.VMEM((images, rows, width), jnp.bfloat16),
            pltpu.VMEM((kv_local, width, 2 * HD), jnp.bfloat16),
            pltpu.VMEM((batch, q_cols), jnp.bfloat16),
            pltpu.VMEM((2, 1, HD), jnp.float32),
            pltpu.VMEM((batch, q_cols), jnp.float32),
            pltpu.VMEM((group_rows, HD), jnp.float32),
            pltpu.VMEM((n_wide, kv_local + 1, group_rows, HD), jnp.bfloat16),
            pltpu.VMEM((total_rows, HD), jnp.int32),
            pltpu.VMEM((total_rows, HD), jnp.int32),
            pltpu.VMEM((kv_local * images, rows, 2 * HD), jnp.float32),
            pltpu.VMEM((kv_local, total_rows, 2 * HD), jnp.float32),
            pltpu.VMEM((kv_local, peers, block, 2 * HD), jnp.bfloat16),
            pltpu.VMEM((kv_local, peers, block, 2 * HD), jnp.bfloat16),
            pltpu.VMEM((block, HD), jnp.float32),
            dma((kv_local, CHUNKS, 2)),
            dma((CHUNKS,)),
            dma((images,)),
            dma((3,)),
            dma((n_wide,)),
            dma((n_wide,)),
            dma((kv_local, peers)),
            dma((kv_local, peers)),
        ],
        compiler_params=pltpu.CompilerParams(
            collective_id=0, has_side_effects=True, vmem_limit_bytes=56 * 1024 * 1024
        ),
    )(
        patch_store,
        w_key,
        w_value,
        key_gain.reshape(1, HD),
        query_gain.reshape(1, HD),
        queries,
        owner_table,
        reader_table,
        request_image,
        image_tiles,
    )


def solution(mesh):
    placed = (
        P("wide", "depth", None),
        P(None, "narrow"),
        P(None, "narrow"),
        P(),
        P(),
        P("wide", "narrow"),
        P(),
        P(),
        P("wide"),
        P(),
    )
    return jax.shard_map(
        functools.partial(local, mesh.shape["wide"], mesh.shape["depth"]),
        mesh=mesh,
        in_specs=placed,
        out_specs=P(("wide", "depth"), "narrow"),
        check_vma=False,
    )
```

time: 63.5 us -> 23.6 us (0.37)
  Pallas kernels: 0 us -> 22 us
  blocking collectives: 19.9 us -> 0 us
  matrix products: 16.1 us -> 0 us
  starting transfers between devices: 7.75 us -> 0 us
  local copies, waits for them, and re-layouts: 8.68 us -> 1.3 us
  waiting for transfers between devices: 7.14 us -> 0 us
  other arithmetic: 3.42 us -> 0 us
    pallas_call x0 -> x1, Pallas kernels: none -> 22 us  [local(): pl.pallas_call(functools.partial(kernel, n_wide, n_depth), out_shape=jax....]
    psum x1 -> x0, blocking collectives: 19.9 us -> none  [local(): lax.psum(denominator.astype(jnp.bfloat16), 'depth').astype(jnp.float32)]
    dot_general x6 -> x0, matrix products: 16.1 us -> none  [the longest x1 6.52 us: local(): jnp.dot(patch_rows, w_value, preferred_element_type=jnp.float32)]
    all_to_all x2 -> x0, starting transfers between devices: 7.75 us -> none  [the longest x1 4.24 us: local(): lax.all_to_all(send_keys, 'wide', split_axis=0, concat_axis=0, tiled=True)]
    all_to_all x2 -> x0, waiting for transfers between devices: 7.14 us -> none  [the longest x1 7.14 us: local(): lax.all_to_all(send_values, 'wide', split_axis=0, concat_axis=0, tiled=True)]
    dot_general x1 -> x0, local copies, waits for them, and re-layouts: 4.27 us -> none  [local(): jnp.dot(patch_rows, w_key, preferred_element_type=jnp.float32)]
    reduce_sum x3 -> x0, other arithmetic: 2.41 us -> none  [the longest x1 1.15 us: local(): jnp.sum(got_keys, axis=0, dtype=jnp.float32).astype(jnp.bfloat16)]
    reshape x5 -> x0, local copies, waits for them, and re-layouts: 2.06 us -> none  [the longest x1 1.44 us: local(): values = values.reshape(images_here, rows_here * kv_cols)]
  transfers between devices with their start and end apart: 2 -> 0, of which waited for: 1 -> 0; matrix products, arithmetic and copies ran while one was open for 19% -> 0% of each run, Pallas kernels for 0% -> 0%
where the time goes in v1:
time: 23.6 us; the launch traced here: 23.3 us
  Pallas kernels  22 us (93%)
  local copies, waits for them, and re-layouts  1.3 us (6%)
    pallas_call x1, Pallas kernels, local(): pl.pallas_call(functools.partial(kernel, n_wide, n_depth), out_shape=jax....  22 us
    unnamed x1, local copies, waits for them, and re-layouts  1.3 us

profile of v1, /device:TPU:0, one launch (start us, length us, event | category | flops | bytes accessed | tf_op | source)
XLA Modules:
  0.0 23.3 jit_solution(1902174903142489324)
XLA Ops:
  0.0 22.0 %shard_map.100 = bf16[4,1024]{1,0:T(4,128)(2,1)} custom-call(bf16[4,256,4096]{2,1,0:T(8,128)(2,1)} %store.1, bf16[4096,256]{1,0:T(8,128)(2,1)} %w_key.1, bf16[4096,256]{1,0:T(8,128)(2,1)} %w_value.1, f32[1,128]{1,0:T(1,128)} %bitcast.2, f32[1,128]{1,0:T(1,128)} %bitcast.3, bf16[16,1024]{1,0:T(8,128)(2,1)} %queries.1, s32[8]{0:T(128)} %owner_table.1, ...), custom_call_target="tpu_custom_call" | custom-call | tf_op jit(solution)/shard_map/pallas_call | solution.py:323
  22.0 1.3 %copy.12 = bf16[4,1024]{1,0:T(4,128)(2,1)} copy(bf16[4,1024]{1,0:T(4,128)(2,1)} %shard_map.100) | data formatting | bytes 16384

commit v2 on v1

--- a/solution.py
+++ b/solution.py
@@ -12,7 +12,7 @@
 TILE_P = 256
 EPSILON = 1e-05
 CHUNKS = 4
-LAG = 3
+MEET = 2
 MESH = pl.DeviceIdType.MESH
 
 
@@ -25,11 +25,15 @@
     key_gain,
     query_gain,
     queries,
+    owner_hbm,
+    reader_hbm,
+    request_hbm,
+    tiles_hbm,
+    out,
     owner_table,
     reader_table,
     request_image,
     image_tiles,
-    out,
     xbuf,
     wbuf,
     qraw,
@@ -40,7 +44,8 @@
     row_slot,
     row_limit,
     raw,
-    acc,
+    keys,
+    values,
     msg,
     got,
     res,
@@ -66,6 +71,21 @@
     wide, depth = lax.axis_index("wide"), lax.axis_index("depth")
     me = wide * n_depth + depth
 
+    barrier = pltpu.get_barrier_semaphore()
+
+    def peer(offset):
+        there = {
+            "wide": lax.rem(wide + offset // n_depth, n_wide),
+            "depth": lax.rem(depth + offset % n_depth, n_depth),
+        }
+        return there["wide"] * n_depth + there["depth"], there
+
+    def greet(offset, carry):
+        pl.semaphore_signal(barrier, inc=1, device_id=peer(offset)[1], device_id_type=MESH)
+        return carry
+
+    lax.fori_loop(1, peers, greet, 0, unroll=peers <= 8)
+
     def weight_copies(k, c):
         piece = pl.ds(c * chunk, chunk)
         return [
@@ -88,6 +108,10 @@
         pltpu.make_async_copy(queries, qraw, q_sem.at[0]),
         pltpu.make_async_copy(query_gain, gains.at[0], q_sem.at[1]),
         pltpu.make_async_copy(key_gain, gains.at[1], q_sem.at[2]),
+        pltpu.make_async_copy(owner_hbm, owner_table, q_sem.at[3]),
+        pltpu.make_async_copy(reader_hbm, reader_table, q_sem.at[4]),
+        pltpu.make_async_copy(request_hbm, request_image, q_sem.at[5]),
+        pltpu.make_async_copy(tiles_hbm, image_tiles, q_sem.at[6]),
     ]
     for c in range(CHUNKS):
         for copy in weight_copies(0, c):
@@ -102,18 +126,6 @@
         for c in range(CHUNKS):
             for copy in weight_copies(k, c):
                 copy.start()
-
-    barrier = pltpu.get_barrier_semaphore()
-
-    def peer(offset):
-        index = lax.rem(me + offset, peers)
-        return index, {"wide": index // n_depth, "depth": lax.rem(index, n_depth)}
-
-    def greet(offset, carry):
-        pl.semaphore_signal(barrier, inc=1, device_id=peer(offset)[1], device_id_type=MESH)
-        return carry
-
-    lax.fori_loop(1, peers, greet, 0, unroll=peers <= 8)
 
     for copy in small:
         copy.wait()
@@ -136,7 +148,6 @@
     for b in range(batch):
         entry = jnp.where(request == b, request_image[b], entry)
     qx[wide, kv_local] = entry.astype(jnp.float32).astype(jnp.bfloat16)
-    acc[...] = jnp.zeros_like(acc)
 
     def query_copy(offset):
         return pltpu.make_async_remote_copy(
@@ -200,25 +211,48 @@
     def wider(tile):
         return jnp.concatenate([tile] * (rows // HD), axis=1) if rows > HD else tile
 
-    def attend(unit):
+    def prepare(unit):
         k, j = divmod(unit, images)
-        keys = raw[unit, :, :HD]
-        mean = jnp.mean(keys * keys, axis=-1, keepdims=True)
-        keys = (keys * lax.rsqrt(mean + EPSILON)).astype(jnp.bfloat16)
-        values = raw[unit, :, HD:].astype(jnp.bfloat16)
-        values = jnp.concatenate([values, jnp.ones_like(values)], axis=1)
-        asked = qx[:, k].reshape(total_rows, HD)
+        span = pl.ds(j * rows, rows)
+        total = raw[unit]
+        head = total[:, :HD]
+        mean = jnp.mean(head * head, axis=-1, keepdims=True)
+        keys[k, span, :] = (head * lax.rsqrt(mean + EPSILON)).astype(jnp.bfloat16)
+        value = total[:, HD:].astype(jnp.bfloat16)
+        values[k, span, :] = jnp.concatenate([value, jnp.ones_like(value)], axis=1)
+
+    def attend_groups(k, start, count):
+        span = pl.ds(start * group_rows, count * group_rows)
+        asked = qx[pl.ds(start, count), k].reshape(count * group_rows, HD)
+        wanted, limits = wider(row_slot[span, :]), wider(row_limit[span, :])
         scores = lax.dot_general(
-            asked, keys, (((1,), (1,)), ((), ())), preferred_element_type=jnp.float32
-        )
-        keep = wider(row_slot[...]) == wide * images + j
-        if not whole_tiles:
-            place = lax.broadcasted_iota(jnp.int32, (total_rows, rows), 1)
-            keep = keep & (place < wider(row_limit[...]))
-        weights = jnp.where(keep, jnp.exp(scores), 0.0).astype(jnp.bfloat16)
-        acc[k] += jnp.dot(weights, values, preferred_element_type=jnp.float32)
-        if j == images - 1:
-            msg[k] = acc[k].astype(jnp.bfloat16).reshape(peers, block, 2 * HD)
+            asked, keys[k], (((1,), (1,)), ((), ())), preferred_element_type=jnp.float32
+        )
+        weights = []
+        for j in range(images):
+            keep = wanted == wide * images + j
+            if not whole_tiles:
+                place = lax.broadcasted_iota(jnp.int32, keep.shape, 1)
+                keep = keep & (place < limits)
+            part = jnp.exp(scores[:, j * rows : (j + 1) * rows])
+            weights.append(jnp.where(keep, part, 0.0).astype(jnp.bfloat16))
+        total = jnp.dot(
+            jnp.concatenate(weights, axis=1), values[k], preferred_element_type=jnp.float32
+        )
+        msg[k, pl.ds(start * n_depth, count * n_depth)] = total.astype(jnp.bfloat16).reshape(
+            count * n_depth, block, 2 * HD
+        )
+
+    def attend(k):
+        if n_wide <= 2:
+            attend_groups(k, 0, n_wide)
+        else:
+
+            def step(g, carry):
+                attend_groups(k, g, 1)
+                return carry
+
+            lax.fori_loop(0, n_wide, step, 0)
 
     def project(unit):
         k, j = divmod(unit, images)
@@ -243,30 +277,19 @@
         raw[unit] = jnp.dot(xbuf[j], wbuf[k], preferred_element_type=jnp.float32)
 
     units = kv_local * images
-    pending, sent, ready = [], 0, []
+    meet = min(MEET, units - 1)
     for unit in range(units):
         project(unit)
-        if unit == 0:
+        if unit > 0:
+            prepare(unit - 1)
+        if unit == meet:
             pl.semaphore_wait(barrier, peers - 1)
             for offset in range(1, n_wide):
                 query_copy(offset).start()
-        for k in ready:
-            send_results(k)
-        ready = []
-        if unit == min(LAG, units - 1):
-            read_queries()
-        if unit >= LAG:
-            for old in pending[:2]:
-                attend(old)
-                if old % images == images - 1:
-                    ready.append(old // images)
-            pending = pending[2:]
-        pending.append(unit)
-    for old in pending:
-        attend(old)
-        if old % images == images - 1:
-            ready.append(old // images)
-    for k in ready:
+    prepare(units - 1)
+    read_queries()
+    for k in range(kv_local):
+        attend(k)
         send_results(k)
 
     for k in range(kv_local):
@@ -318,14 +341,17 @@
     peers = n_wide * n_depth
     total_rows = peers * block
     anywhere = pl.BlockSpec(memory_space=pl.ANY)
-    scalars = pl.BlockSpec(memory_space=pltpu.SMEM)
     dma = pltpu.SemaphoreType.DMA
     return pl.pallas_call(
         functools.partial(kernel, n_wide, n_depth),
         out_shape=jax.ShapeDtypeStruct((share, q_cols), jnp.bfloat16),
-        in_specs=[anywhere] * 6 + [scalars] * 4,
+        in_specs=[anywhere] * 10,
         out_specs=pl.BlockSpec(memory_space=pltpu.VMEM),
         scratch_shapes=[
+            pltpu.SMEM(owner_table.shape, jnp.int32),
+            pltpu.SMEM(reader_table.shape, jnp.int32),
+            pltpu.SMEM(request_image.shape, jnp.int32),
+            pltpu.SMEM(image_tiles.shape, jnp.int32),
             pltpu.VMEM((images, rows, width), jnp.bfloat16),
             pltpu.VMEM((kv_local, width, 2 * HD), jnp.bfloat16),
             pltpu.VMEM((batch, q_cols), jnp.bfloat16),
@@ -336,14 +362,15 @@
             pltpu.VMEM((total_rows, HD), jnp.int32),
             pltpu.VMEM((total_rows, HD), jnp.int32),
             pltpu.VMEM((kv_local * images, rows, 2 * HD), jnp.float32),
-            pltpu.VMEM((kv_local, total_rows, 2 * HD), jnp.float32),
+            pltpu.VMEM((kv_local, images * rows, HD), jnp.bfloat16),
+            pltpu.VMEM((kv_local, images * rows, 2 * HD), jnp.bfloat16),
             pltpu.VMEM((kv_local, peers, block, 2 * HD), jnp.bfloat16),
             pltpu.VMEM((kv_local, peers, block, 2 * HD), jnp.bfloat16),
             pltpu.VMEM((block, HD), jnp.float32),
             dma((kv_local, CHUNKS, 2)),
             dma((CHUNKS,)),
             dma((images,)),
-            dma((3,)),
+            dma((7,)),
             dma((n_wide,)),
             dma((n_wide,)),
             dma((kv_local, peers)),

time: 23.6 us -> 21.2 us (0.90)
  Pallas kernels: 22 us -> 19.7 us
    pallas_call x1, Pallas kernels: 22 us -> 19.7 us  [local(): pl.pallas_call(functools.partial(kernel, n_wide, n_depth), out_shape=jax....]
where the time goes in v2:
time: 21.2 us; the launch traced here: 21 us
  Pallas kernels  19.7 us (93%)
  local copies, waits for them, and re-layouts  1.3 us (6%)
    pallas_call x1, Pallas kernels, local(): pl.pallas_call(functools.partial(kernel, n_wide, n_depth), out_shape=jax....  19.7 us
    unnamed x1, local copies, waits for them, and re-layouts  1.3 us

profile of v2, /device:TPU:0, one launch (start us, length us, event | category | flops | bytes accessed | tf_op | source)
XLA Modules:
  0.0 21.0 jit_solution(9481707826616593841)
XLA Ops:
  0.0 19.7 %shard_map.100 = bf16[4,1024]{1,0:T(4,128)(2,1)} custom-call(bf16[4,256,4096]{2,1,0:T(8,128)(2,1)} %store.1, bf16[4096,256]{1,0:T(8,128)(2,1)} %w_key.1, bf16[4096,256]{1,0:T(8,128)(2,1)} %w_value.1, f32[1,128]{1,0:T(1,128)} %bitcast.2, f32[1,128]{1,0:T(1,128)} %bitcast.3, bf16[16,1024]{1,0:T(8,128)(2,1)} %queries.1, s32[8]{0:T(128)} %owner_hbm.1, ...), custom_call_target="tpu_custom_call" | custom-call | tf_op jit(solution)/shard_map/pallas_call | solution.py:345
  19.7 1.3 %copy.12 = bf16[4,1024]{1,0:T(4,128)(2,1)} copy(bf16[4,1024]{1,0:T(4,128)(2,1)} %shard_map.100) | data formatting | bytes 16384

commit v3 on v2

--- a/solution.py
+++ b/solution.py
@@ -12,7 +12,7 @@
 TILE_P = 256
 EPSILON = 1e-05
 CHUNKS = 4
-MEET = 2
+MEET = 1
 MESH = pl.DeviceIdType.MESH
 
 
@@ -50,7 +50,6 @@
     got,
     res,
     w_sem,
-    x0_sem,
     x_sem,
     q_sem,
     q_send,
@@ -97,12 +96,9 @@
             for part, source in enumerate((w_key, w_value))
         ]
 
-    def first_copy(c):
+    def patch_copy(c):
         piece = pl.ds(c * chunk, chunk)
-        return pltpu.make_async_copy(store.at[0, :, piece], xbuf.at[0, :, piece], x0_sem.at[c])
-
-    def image_copy(j):
-        return pltpu.make_async_copy(store.at[j], xbuf.at[j], x_sem.at[j])
+        return pltpu.make_async_copy(store.at[:, :, piece], xbuf.at[:, :, piece], x_sem.at[c])
 
     small = [
         pltpu.make_async_copy(queries, qraw, q_sem.at[0]),
@@ -114,17 +110,12 @@
         pltpu.make_async_copy(tiles_hbm, image_tiles, q_sem.at[6]),
     ]
     for c in range(CHUNKS):
-        for copy in weight_copies(0, c):
-            copy.start()
-        first_copy(c).start()
+        for k in range(kv_local):
+            for copy in weight_copies(k, c):
+                copy.start()
+        patch_copy(c).start()
         if c == 0:
             for copy in small:
-                copy.start()
-    for j in range(1, images):
-        image_copy(j).start()
-    for k in range(1, kv_local):
-        for c in range(CHUNKS):
-            for copy in weight_copies(k, c):
                 copy.start()
 
     for copy in small:
@@ -211,15 +202,13 @@
     def wider(tile):
         return jnp.concatenate([tile] * (rows // HD), axis=1) if rows > HD else tile
 
-    def prepare(unit):
-        k, j = divmod(unit, images)
-        span = pl.ds(j * rows, rows)
-        total = raw[unit]
+    def prepare(k):
+        total = raw[k]
         head = total[:, :HD]
         mean = jnp.mean(head * head, axis=-1, keepdims=True)
-        keys[k, span, :] = (head * lax.rsqrt(mean + EPSILON)).astype(jnp.bfloat16)
+        keys[k] = (head * lax.rsqrt(mean + EPSILON)).astype(jnp.bfloat16)
         value = total[:, HD:].astype(jnp.bfloat16)
-        values[k, span, :] = jnp.concatenate([value, jnp.ones_like(value)], axis=1)
+        values[k] = jnp.concatenate([value, jnp.ones_like(value)], axis=1)
 
     def attend_groups(k, start, count):
         span = pl.ds(start * group_rows, count * group_rows)
@@ -254,39 +243,28 @@
 
             lax.fori_loop(0, n_wide, step, 0)
 
-    def project(unit):
-        k, j = divmod(unit, images)
-        if unit == 0:
-            total = jnp.zeros((rows, 2 * HD), jnp.float32)
-            for c in range(CHUNKS):
-                for copy in weight_copies(0, c):
-                    copy.wait()
-                first_copy(c).wait()
-                piece = pl.ds(c * chunk, chunk)
-                total = total + jnp.dot(
-                    xbuf[0, :, piece], wbuf[0, piece, :], preferred_element_type=jnp.float32
-                )
-            raw[unit] = total
-            return
-        if k == 0:
-            image_copy(j).wait()
-        elif j == 0:
-            for c in range(CHUNKS):
-                for copy in weight_copies(k, c):
-                    copy.wait()
-        raw[unit] = jnp.dot(xbuf[j], wbuf[k], preferred_element_type=jnp.float32)
-
-    units = kv_local * images
-    meet = min(MEET, units - 1)
-    for unit in range(units):
-        project(unit)
-        if unit > 0:
-            prepare(unit - 1)
-        if unit == meet:
+    def project(k, c):
+        piece = pl.ds(c * chunk, chunk)
+        part = jnp.dot(
+            xbuf[:, :, piece].reshape(images * rows, chunk),
+            wbuf[k, piece, :],
+            preferred_element_type=jnp.float32,
+        )
+        raw[k] = part if c == 0 else raw[k] + part
+
+    for c in range(CHUNKS):
+        for k in range(kv_local):
+            for copy in weight_copies(k, c):
+                copy.wait()
+        patch_copy(c).wait()
+        for k in range(kv_local):
+            project(k, c)
+            if c == CHUNKS - 1:
+                prepare(k)
+        if c == min(MEET, CHUNKS - 1):
             pl.semaphore_wait(barrier, peers - 1)
             for offset in range(1, n_wide):
                 query_copy(offset).start()
-    prepare(units - 1)
     read_queries()
     for k in range(kv_local):
         attend(k)
@@ -361,7 +339,7 @@
             pltpu.VMEM((n_wide, kv_local + 1, group_rows, HD), jnp.bfloat16),
             pltpu.VMEM((total_rows, HD), jnp.int32),
             pltpu.VMEM((total_rows, HD), jnp.int32),
-            pltpu.VMEM((kv_local * images, rows, 2 * HD), jnp.float32),
+            pltpu.VMEM((kv_local, images * rows, 2 * HD), jnp.float32),
             pltpu.VMEM((kv_local, images * rows, HD), jnp.bfloat16),
             pltpu.VMEM((kv_local, images * rows, 2 * HD), jnp.bfloat16),
             pltpu.VMEM((kv_local, peers, block, 2 * HD), jnp.bfloat16),
@@ -369,7 +347,6 @@
             pltpu.VMEM((block, HD), jnp.float32),
             dma((kv_local, CHUNKS, 2)),
             dma((CHUNKS,)),
-            dma((images,)),
             dma((7,)),
             dma((n_wide,)),
             dma((n_wide,)),

time: 21.2 us -> 19.2 us (0.906)
  Pallas kernels: 19.7 us -> 17.7 us
    pallas_call x1, Pallas kernels: 19.7 us -> 17.7 us  [local(): pl.pallas_call(functools.partial(kernel, n_wide, n_depth), out_shape=jax....]
where the time goes in v3:
time: 19.2 us; the launch traced here: 19 us
  Pallas kernels  17.7 us (92%)
  local copies, waits for them, and re-layouts  1.3 us (7%)
    pallas_call x1, Pallas kernels, local(): pl.pallas_call(functools.partial(kernel, n_wide, n_depth), out_shape=jax....  17.7 us
    unnamed x1, local copies, waits for them, and re-layouts  1.3 us

profile of v3, /device:TPU:0, one launch (start us, length us, event | category | flops | bytes accessed | tf_op | source)
XLA Modules:
  0.0 19.0 jit_solution(3067670877875506115)
XLA Ops:
  0.0 17.7 %shard_map.100 = bf16[4,1024]{1,0:T(4,128)(2,1)} custom-call(bf16[4,256,4096]{2,1,0:T(8,128)(2,1)} %store.1, bf16[4096,256]{1,0:T(8,128)(2,1)} %w_key.1, bf16[4096,256]{1,0:T(8,128)(2,1)} %w_value.1, f32[1,128]{1,0:T(1,128)} %bitcast.2, f32[1,128]{1,0:T(1,128)} %bitcast.3, bf16[16,1024]{1,0:T(8,128)(2,1)} %queries.1, s32[8]{0:T(128)} %owner_hbm.1, ...), custom_call_target="tpu_custom_call" | custom-call | tf_op jit(solution)/shard_map/pallas_call | solution.py:323
  17.7 1.3 %copy.12 = bf16[4,1024]{1,0:T(4,128)(2,1)} copy(bf16[4,1024]{1,0:T(4,128)(2,1)} %shard_map.100) | data formatting | bytes 16384

commit v4 on v3

--- a/solution.py
+++ b/solution.py
@@ -12,7 +12,7 @@
 TILE_P = 256
 EPSILON = 1e-05
 CHUNKS = 4
-MEET = 1
+MEET = 0
 MESH = pl.DeviceIdType.MESH
 
 
@@ -69,6 +69,7 @@
     chunk = width // CHUNKS
     wide, depth = lax.axis_index("wide"), lax.axis_index("depth")
     me = wide * n_depth + depth
+    part_lanes = HD // kv_local
 
     barrier = pltpu.get_barrier_semaphore()
 
@@ -161,20 +162,20 @@
             device_id_type=MESH,
         )
 
-    def result_copy(k, offset):
+    def result_copy(offset):
         index, device = peer(offset)
         return pltpu.make_async_remote_copy(
-            src_ref=msg.at[k, index],
-            dst_ref=got.at[k, offset],
-            send_sem=m_send.at[k, offset],
-            recv_sem=m_recv.at[k, offset],
+            src_ref=msg.at[index],
+            dst_ref=got.at[offset],
+            send_sem=m_send.at[offset],
+            recv_sem=m_recv.at[offset],
             device_id=device,
             device_id_type=MESH,
         )
 
-    def send_results(k):
+    def send_results():
         def step(offset, carry):
-            result_copy(k, offset).start()
+            result_copy(offset).start()
             return carry
 
         lax.fori_loop(1, peers, step, 0, unroll=peers <= 8)
@@ -228,9 +229,15 @@
         total = jnp.dot(
             jnp.concatenate(weights, axis=1), values[k], preferred_element_type=jnp.float32
         )
-        msg[k, pl.ds(start * n_depth, count * n_depth)] = total.astype(jnp.bfloat16).reshape(
-            count * n_depth, block, 2 * HD
-        )
+        total = total.astype(jnp.bfloat16).reshape(count * n_depth, block, 2 * HD)
+        dest = pl.ds(start * n_depth, count * n_depth)
+        msg[dest, k] = total[:, :, :HD]
+        below = total[:, :, HD:]
+        if k:
+            lane = lax.broadcasted_iota(jnp.int32, below.shape, 2)
+            older = msg[dest, kv_local].astype(jnp.float32)
+            below = jnp.where(lane < k * part_lanes, older, below.astype(jnp.float32))
+        msg[dest, kv_local] = below.astype(jnp.bfloat16)
 
     def attend(k):
         if n_wide <= 2:
@@ -268,17 +275,17 @@
     read_queries()
     for k in range(kv_local):
         attend(k)
-        send_results(k)
-
+    send_results()
+
+    total = msg[me].astype(jnp.float32)
+
+    def collect(offset, total):
+        result_copy(offset).wait_recv()
+        return total + got[offset].astype(jnp.float32)
+
+    total = lax.fori_loop(1, peers, collect, total, unroll=peers <= 8)
     for k in range(kv_local):
-        total = msg[k, me].astype(jnp.float32)
-
-        def collect(offset, total, k=k):
-            result_copy(k, offset).wait_recv()
-            return total + got[k, offset].astype(jnp.float32)
-
-        total = lax.fori_loop(1, peers, collect, total, unroll=peers <= 8)
-        res[...] = total[:, :HD] / total[:, HD:]
+        res[...] = total[k] / total[kv_local, :, k * part_lanes : k * part_lanes + 1]
         for g in range(group):
             out[:, pl.ds((k * group + g) * HD, HD)] = res[pl.ds(g * share, share), :].astype(
                 out.dtype
@@ -286,13 +293,12 @@
 
     for offset in range(1, n_wide):
         query_copy(offset).wait_send()
-    for k in range(kv_local):
-
-        def drain(offset, carry, k=k):
-            result_copy(k, offset).wait_send()
-            return carry
-
-        lax.fori_loop(1, peers, drain, 0, unroll=peers <= 8)
+
+    def drain(offset, carry):
+        result_copy(offset).wait_send()
+        return carry
+
+    lax.fori_loop(1, peers, drain, 0, unroll=peers <= 8)
 
 
 def local(
@@ -322,7 +328,7 @@
     dma = pltpu.SemaphoreType.DMA
     return pl.pallas_call(
         functools.partial(kernel, n_wide, n_depth),
-        out_shape=jax.ShapeDtypeStruct((share, q_cols), jnp.bfloat16),
+        out_shape=pltpu.VMEM((share, q_cols), jnp.bfloat16),
         in_specs=[anywhere] * 10,
         out_specs=pl.BlockSpec(memory_space=pltpu.VMEM),
         scratch_shapes=[
@@ -342,16 +348,16 @@
             pltpu.VMEM((kv_local, images * rows, 2 * HD), jnp.float32),
             pltpu.VMEM((kv_local, images * rows, HD), jnp.bfloat16),
             pltpu.VMEM((kv_local, images * rows, 2 * HD), jnp.bfloat16),
-            pltpu.VMEM((kv_local, peers, block, 2 * HD), jnp.bfloat16),
-            pltpu.VMEM((kv_local, peers, block, 2 * HD), jnp.bfloat16),
+            pltpu.VMEM((peers, kv_local + 1, block, HD), jnp.bfloat16),
+            pltpu.VMEM((peers, kv_local + 1, block, HD), jnp.bfloat16),
             pltpu.VMEM((block, HD), jnp.float32),
             dma((kv_local, CHUNKS, 2)),
             dma((CHUNKS,)),
             dma((7,)),
             dma((n_wide,)),
             dma((n_wide,)),
-            dma((kv_local, peers)),
-            dma((kv_local, peers)),
+            dma((peers,)),
+            dma((peers,)),
         ],
         compiler_params=pltpu.CompilerParams(
             collective_id=0, has_side_effects=True, vmem_limit_bytes=56 * 1024 * 1024

time: 19.2 us -> 17.3 us (0.901)
  Pallas kernels: 17.7 us -> 16.6 us
  local copies, waits for them, and re-layouts: 1.3 us -> 0.6 us
    pallas_call x1, Pallas kernels: 17.7 us -> 16.6 us  [local(): pl.pallas_call(functools.partial(kernel, n_wide, n_depth), out_shape=pltp...]
    unnamed x1, local copies, waits for them, and re-layouts: 1.3 us -> 0.6 us
where the time goes in v4:
time: 17.3 us; the launch traced here: 17.2 us
  Pallas kernels  16.6 us (96%)
  local copies, waits for them, and re-layouts  0.6 us (3%)
    pallas_call x1, Pallas kernels, local(): pl.pallas_call(functools.partial(kernel, n_wide, n_depth), out_shape=pltp...  16.6 us
    unnamed x1, local copies, waits for them, and re-layouts  0.6 us

profile of v4, /device:TPU:0, one launch (start us, length us, event | category | flops | bytes accessed | tf_op | source)
XLA Modules:
  0.0 17.2 jit_solution(6190802467928955704)
XLA Ops:
  0.0 16.6 %shard_map.100 = bf16[4,1024]{1,0:T(4,128)(2,1)S(1)} custom-call(bf16[4,256,4096]{2,1,0:T(8,128)(2,1)} %store.1, bf16[4096,256]{1,0:T(8,128)(2,1)} %w_key.1, bf16[4096,256]{1,0:T(8,128)(2,1)} %w_value.1, f32[1,128]{1,0:T(1,128)} %bitcast.2, f32[1,128]{1,0:T(1,128)} %bitcast.3, bf16[16,1024]{1,0:T(8,128)(2,1)} %queries.1, s32[8]{0:T(128)} %owner_hbm.1, ...), custom_call_target="tpu_custom_call" | custom-call | tf_op jit(solution)/shard_map/pallas_call | solution.py:329
  16.6 0.6 %copy.12 = bf16[4,1024]{1,0:T(4,128)(2,1)} copy(bf16[4,1024]{1,0:T(4,128)(2,1)S(1)} %shard_map.100) | data formatting | bytes 16384
